TPU v7x, 32 devices: a whole 2x2x4 slice. The times are simulated.
32 devices in a mesh: rep: 4 (over z), tp: 8 (over y, x, core).
Axes of the slice: x: 2, y: 2, z: 4, core: 2. Of those that a mesh axis runs over, the one named last changes fastest.
Arguments:
- attn: bfloat16 [3072, 4096], P('rep', 'tp'), parts along dimension 0, may hold values from -6 to 6
- output_weight: bfloat16 [4096, 8192], P(None, 'tp'), may hold values from -0.09375 to 0.09375
- adapter_down_weight: bfloat16 [8, 64, 4096], P('tp'), may hold values from -0.09375 to 0.09375
- adapter_up_weight: bfloat16 [8, 64, 8192], P('tp'), may hold values from -0.75 to 0.75
- block_adapter_index: int32 [24], P('rep'), parts along dimension 0, may hold values from 0 to 7
- adapter_page_table: int32 [8], replicated, may hold values from 0 to 7, each once
Outputs:
- projected: bfloat16 [3072, 8192], P('rep', 'tp'), parts along dimension 0
There are 4 independent parts, one for each index of `rep`. A program takes and returns all parts, laid end to end along the dimension named above; an argument that names none is the same for every part. Nothing has to cross between parts.
Inputs may be any that keep to these rules, and one draw needn't show every extreme that they name: adapter_page_table is a permutation; adapter a is stored on tp device adapter_page_table[a] (each device holds exactly one adapter), and row adapter_page_table[a] of adapter_down_weight and adapter_up_weight holds it. `block_adapter_index`: the adapter used by all 128 tokens of a block.
All inputs are finite; a program needn't handle non-finite values.
Results may differ from a plain program's by a relative error of at most 0.0046.
Values may be sent and summed in bfloat16 or wider, within the bound.
A program may use at most 64 MiB of HBM per device.

v0:
```python
import jax
import jax.numpy as jnp
from jax import lax
from jax.sharding import PartitionSpec as P

adapter_scale = 2.0


def shards(
    attn,
    output_weight,
    adapter_down_weight,
    adapter_up_weight,
    block_adapter_index,
    adapter_page_table,
):
    tokens = attn.shape[0]
    blocks = block_adapter_index.shape[0]
    block_rows = tokens // blocks
    page_slot_count = adapter_down_weight.shape[0]
    pool_size = adapter_page_table.shape[0]
    width_out = output_weight.shape[1]
    position = lax.axis_index("tp")
    matches = block_adapter_index[:, None] == jnp.arange(pool_size, dtype=jnp.int32)[None, :]
    block_page_index = jnp.sum(jnp.where(matches, adapter_page_table[None, :], 0), axis=1)
    up_weight_columns = lax.all_to_all(
        adapter_up_weight, "tp", split_axis=2, concat_axis=0, tiled=True
    )
    block_up = up_weight_columns[block_page_index]
    shard_piece = lax.all_gather(attn, "tp", axis=1, tiled=True)
    base_output = jnp.dot(shard_piece, output_weight, preferred_element_type=jnp.float32)
    row_blocks = shard_piece.reshape(blocks, block_rows, shard_piece.shape[1])
    base_output, side_sum = (
        base_output,
        jnp.einsum(
            "btf,srf->bsrt", row_blocks, adapter_down_weight, preferred_element_type=jnp.float32
        ),
    )
    own_pages = position * page_slot_count + jnp.arange(page_slot_count, dtype=jnp.int32)
    owned = (block_page_index[:, None] == own_pages[None, :]).astype(jnp.float32)
    local_term = jnp.sum(owned[:, :, None, None] * side_sum, axis=1)
    shrunk = lax.psum(local_term.astype(jnp.bfloat16), "tp")
    adapter_output = jnp.einsum(
        "brt,brc->btc", shrunk, block_up, preferred_element_type=jnp.float32
    )
    adapter_output = adapter_output.reshape(tokens, width_out)
    return (base_output + adapter_scale * adapter_output).astype(jnp.bfloat16)


def solution(mesh):
    return jax.shard_map(
        shards,
        mesh=mesh,
        in_specs=(
            P("rep", "tp"),
            P(None, "tp"),
            P("tp", None, None),
            P("tp", None, None),
            P("rep"),
            P(),
        ),
        out_specs=P("rep", "tp"),
        check_vma=False,
    )
```

profile of v0, /device:TPU:0, one launch (start us, length us, event | category | flops | bytes accessed | tf_op | source)
XLA Modules:
  0.0 150.3 jit_solution(16534256131757500711)
XLA Ops:
  6.5 0.0 copy-start
  6.5 0.0 all-gather.2.cloned.1.call-start
  6.5 0.7 all-gather.2.cloned.1.call-update
  7.3 9.2 %copy.11 = bf16[1,64,8192]{1,0,2:T(2,128)(2,1)} copy(bf16[1,64,8192]{2,1,0:T(8,128)(2,1)} %param.9) | data formatting | bytes 2097152 | tf_op args[3]
  16.4 0.5 broadcast.42
  16.9 45.3 %reduce = bf16[8192,64]{1,0:T(8,128)(2,1)S(1)} reduce(bf16[8192,1,64]{2,1,0:T(2,128)(2,1)} %bitcast.36, bf16[]{:T(256)} %broadcast.42), dimensions={1}, to_apply=%bitcast.29.reduce_sub_computation | reduce | bytes 2097154
  62.2 0.0 copy-start.1
  62.2 0.0 copy-start.2
  62.2 2.7 %reshape.51 = bf16[8,2,32768]{2,1,0:T(2,128)(2,1)} reshape(bf16[8192,64]{1,0:T(8,128)(2,1)S(1)} %reduce) | data formatting | bytes 2097152
  64.9 5.2 %all-to-all-start = ((bf16[8,2,32768]{2,1,0:T(2,128)(2,1)}), bf16[8,2,32768]{2,1,0:T(2,128)(2,1)S(1)}, u32[]{:S(2)}, u32[]{:S(2)}) async-start(bf16[8,2,32768]{2,1,0:T(2,128)(2,1)} %reshape.51), calls=%async_computation | async-start | bytes 2097152 | tf_op jit(solution)/shard_map/all_to_all | solution.py:26
  70.1 0.2 all-reduce.2.cloned.1.call-start
  70.3 0.0 copy-done.1
  70.3 0.0 copy-done.2
  70.4 0.2 select_reduce_fusion
  70.6 0.0 all-gather.2.cloned.1.call-done
  70.6 0.0 copy-done
  70.6 5.5 %fusion.3 = bf16[6,64,128]{2,1,0:T(8,128)(2,1)} fusion(bf16[6,128,4096]{2,1,0:T(8,128)(2,1)} %bitcast.39, bf16[1,64,4096]{2,1,0:T(8,128)(2,1)S(1)} %copy-done, f32[6]{0:T(128)S(1)} %compare_convert_fusion), kind=kOutput, calls=%fused_computation.7 | convolution fusion | flops 402751488 | bytes 6914072 | tf_op jit(solution)/shard_map/btf,srf->bsrt/dot_general | solution.py:35
  76.0 0.0 all-reduce.2.cloned.1.call-update
  76.1 9.4 %all-to-all-done = bf16[8,2,32768]{2,1,0:T(2,128)(2,1)S(1)} async-done(((bf16[8,2,32768]{2,1,0:T(2,128)(2,1)}), bf16[8,2,32768]{2,1,0:T(2,128)(2,1)S(1)}, u32[]{:S(2)}, u32[]{:S(2)}) %all-to-all-start) | async-done | bytes 1048608 | tf_op jit(solution)/shard_map/all_to_all | solution.py:26
  85.5 4.3 %reshape.52 = bf16[8192,1,64]{2,1,0:T(2,128)(2,1)} reshape(bf16[8,2,32768]{2,1,0:T(2,128)(2,1)S(1)} %all-to-all-done) | data formatting | bytes 2097152
  89.9 2.5 %copy.16 = bf16[1,64,8192]{1,2,0:T(8,128)(2,1)S(1)} copy(bf16[1,64,8192]{1,0,2:T(2,128)(2,1)} %bitcast.37) | data formatting | bytes 2097152
  92.3 1.6 %copy.13 = bf16[1,64,8,1024]{3,1,2,0:T(8,128)(2,1)} copy(bf16[1,64,8,1024]{1,3,2,0:T(8,128)(2,1)S(1)} %bitcast.38) | data formatting | bytes 2097152 | tf_op jit(solution)/shard_map/all_to_all | solution.py:26
  93.9 1.8 %gather_fusion = bf16[6,64,1024]{2,1,0:T(8,128)(2,1)S(1)} fusion(bf16[8,64,1024]{2,1,0:T(8,128)(2,1)} %bitcast.40, s32[1024]{0:T(1024)S(1)} %pad_clamp_fusion), kind=kCustom, calls=%fused_computation | custom fusion | bytes 1572888 | tf_op jit(solution)/shard_map/gather | solution.py:29
  95.8 34.1 %all-reduce.2.cloned.1.call-done = bf16[6,64,128]{2,1,0:T(8,128)(2,1)} async-done(((bf16[6,64,128]{2,1,0:T(8,128)(2,1)}), bf16[6,64,128]{2,1,0:T(8,128)(2,1)}) %all-reduce.2.cloned.1.call-update) | async-done | bytes 98320 | tf_op jit(solution)/shard_map/psum | solution.py:42
  129.9 1.5 %convolution_multiply_fusion = f32[6,128,1024]{2,1,0:T(8,128)S(1)} fusion(bf16[6,64,128]{2,1,0:T(8,128)(2,1)} %all-reduce.2.cloned.1.call-done, bf16[6,64,1024]{2,1,0:T(8,128)(2,1)S(1)} %gather_fusion), kind=kOutput, calls=%fused_computation.3 | convolution fusion | flops 101449728 | bytes 4030464 | tf_op jit(solution)/shard_map/brt,brc->btc/dot_general | solution.py:43
  131.4 12.1 %fusion = bf16[768,1024]{1,0:T(8,128)(2,1)} fusion(f32[6,128,1024]{2,1,0:T(8,128)S(1)} %convolution_multiply_fusion, bf16[768,4096]{1,0:T(8,128)(2,1)} %all-gather.2.cloned.1.call-done, bf16[4096,1024]{1,0:T(8,128)(2,1)} %param.7), kind=kOutput, calls=%fused_computation.2 | convolution fusion | flops 6444023808 | bytes 19398656 | tf_op jit(solution)/shard_map/dot_general | solution.py:31
  (3 shorter events, 0.0 us)
Async XLA Ops:
  6.5 64.1 %copy-start = (bf16[1,64,4096]{2,1,0:T(8,128)(2,1)S(1)}, bf16[1,64,4096]{2,1,0:T(8,128)(2,1)}, u32[]{:S(2)}) copy-start(bf16[1,64,4096]{2,1,0:T(8,128)(2,1)} %param.8) | copy-start | bytes 1572868
  6.5 64.0 %all-gather.2.cloned.1.call-start = ((), (), s32[]{:S(2)}) async-start(), calls=%async_computation.1 | async-start | bytes 7077888 | tf_op jit(solution)/shard_map/all_gather | solution.py:30
  62.2 8.1 %copy-start.1 = (s32[8]{0:T(128)S(1)}, s32[8]{0:T(128)}, u32[]{:S(2)}) copy-start(s32[8]{0:T(128)} %param.11) | copy-start | bytes 100
  62.2 8.1 %copy-start.2 = (s32[6]{0:T(128)S(1)}, s32[6]{0:T(128)}, u32[]{:S(2)}) copy-start(s32[6]{0:T(128)} %param.10) | copy-start | bytes 76
  64.9 20.6 %all-to-all-start = ((bf16[8,2,32768]{2,1,0:T(2,128)(2,1)}), bf16[8,2,32768]{2,1,0:T(2,128)(2,1)S(1)}, u32[]{:S(2)}, u32[]{:S(2)}) async-start(bf16[8,2,32768]{2,1,0:T(2,128)(2,1)} %reshape.51), calls=%async_computation | async-start | bytes 2097152 | tf_op jit(solution)/shard_map/all_to_all | solution.py:26
  70.1 59.7 %all-reduce.2.cloned.1.call-start = ((), (), s32[]{:S(2)}) async-start(), calls=%async_computation.2 | async-start | bytes 196608 | tf_op jit(solution)/shard_map/psum | solution.py:42
Sparse Core Ops, SparseCore 0:
  9.2 49.2 all-gather.1
  76.2 53.6 all-reduce.1
where the time goes:
time: 151 us; the launch traced here: 150 us
  other arithmetic  45.5 us (30%)
  waiting for transfers between devices  44.3 us (29%)
  local copies, waits for them, and re-layouts  22.6 us (15%)
  matrix products  19.1 us (13%)
  between operations  13.5 us (9%)
  starting transfers between devices  5.45 us (4%)
    unnamed x1, other arithmetic  45.3 us
    psum x1, waiting for transfers between devices, shards(): shrunk = lax.psum(local_term.astype(jnp.bfloat16), 'tp')  34.1 us
    unnamed x11, local copies, waits for them, and re-layouts  19.2 us
    dot_general x1, matrix products, shards(): jnp.dot(shard_piece, output_weight, preferred_element_type=jnp.float32)  12.1 us
    all_to_all x1, waiting for transfers between devices, shards(): lax.all_to_all(adapter_up_weight, 'tp', split_axis=2, concat_axis=0, tile...  9.44 us
    dot_general x1, matrix products, shards(): jnp.einsum('btf,srf->bsrt', row_blocks, adapter_down_weight, preferred_el...  5.45 us
    all_to_all x1, starting transfers between devices, shards(): lax.all_to_all(adapter_up_weight, 'tp', split_axis=2, concat_axis=0, tile...  5.23 us
  transfers between devices with their start and end apart: 3, of which 2 were waited for; matrix products, arithmetic and copies ran while one was open for 49% of the time, Pallas kernels for 0%

commit v1 on v0

--- a/solution.py
+++ b/solution.py
@@ -4,6 +4,13 @@
 from jax.sharding import PartitionSpec as P
 
 adapter_scale = 2.0
+
+
+def swap_blocks(x, name, split, join):
+    n_dev = lax.axis_size(name)
+    shards = jnp.stack(jnp.split(x, n_dev, axis=split), axis=0)
+    shards = lax.all_to_all(shards, name, split_axis=0, concat_axis=0)
+    return jnp.concatenate(shards, axis=join)
 
 
 def shards(
@@ -23,9 +30,7 @@
     position = lax.axis_index("tp")
     matches = block_adapter_index[:, None] == jnp.arange(pool_size, dtype=jnp.int32)[None, :]
     block_page_index = jnp.sum(jnp.where(matches, adapter_page_table[None, :], 0), axis=1)
-    up_weight_columns = lax.all_to_all(
-        adapter_up_weight, "tp", split_axis=2, concat_axis=0, tiled=True
-    )
+    up_weight_columns = swap_blocks(adapter_up_weight, "tp", 2, 0)
     block_up = up_weight_columns[block_page_index]
     shard_piece = lax.all_gather(attn, "tp", axis=1, tiled=True)
     base_output = jnp.dot(shard_piece, output_weight, preferred_element_type=jnp.float32)

time: 151 us -> 145 us (0.960)
  waiting for transfers between devices: 44.3 us -> 93.2 us
  other arithmetic: 45.5 us -> 0.87 us
  local copies, waits for them, and re-layouts: 22.6 us -> 13.2 us
    unnamed x1 -> x0, other arithmetic: 45.3 us -> none
    all_gather x1, waiting for transfers between devices: 0.02 us -> 40.9 us  [shards(): shard_piece = lax.all_gather(attn, 'tp', axis=1, tiled=True)]
    psum x1, waiting for transfers between devices: 34.1 us -> 51.6 us  [shards(): shrunk = lax.psum(local_term.astype(jnp.bfloat16), 'tp')]
    all_to_all x1, waiting for transfers between devices: 9.44 us -> 0.01 us  [swap_blocks(): shards = lax.all_to_all(shards, name, split_axis=0, concat_axis=0)]
    unnamed x11 -> x9, local copies, waits for them, and re-layouts: 19.2 us -> 11 us
    all_to_all x1 -> x0, local copies, waits for them, and re-layouts: 1.61 us -> none  [shards(): lax.all_to_all(adapter_up_weight, 'tp', split_axis=2, concat_axis=0, tile...]
    another operation x0 -> x1, local copies, waits for them, and re-layouts: none -> 1.58 us  [swap_blocks(): shards = jnp.stack(jnp.split(x, n_dev, axis=split), axis=0)]
  transfers between devices with their start and end apart: 3 -> 3, of which waited for: 2 -> 2; matrix products, arithmetic and copies ran while one was open for 49% -> 13% of each run, Pallas kernels for 0% -> 0%
where the time goes in v1:
time: 145 us
  waiting for transfers between devices  93.2 us (64%)
  matrix products  19 us (13%)
  between operations  13.4 us (9%)
  local copies, waits for them, and re-layouts  13.2 us (9%)
  starting transfers between devices  5.25 us (4%)
    psum x1, waiting for transfers between devices, shards(): shrunk = lax.psum(local_term.astype(jnp.bfloat16), 'tp')  51.6 us
    all_gather x1, waiting for transfers between devices, shards(): shard_piece = lax.all_gather(attn, 'tp', axis=1, tiled=True)  40.9 us
    dot_general x1, matrix products, shards(): jnp.dot(shard_piece, output_weight, preferred_element_type=jnp.float32)  12.1 us
    unnamed x9, local copies, waits for them, and re-layouts  11 us
    dot_general x1, matrix products, shards(): jnp.einsum('btf,srf->bsrt', row_blocks, adapter_down_weight, preferred_el...  5.45 us
    all_to_all x1, starting transfers between devices, swap_blocks(): shards = lax.all_to_all(shards, name, split_axis=0, concat_axis=0)  5.22 us
  transfers between devices with their start and end apart: 3, of which 2 were waited for; matrix products, arithmetic and copies ran while one was open for 13% of the time, Pallas kernels for 0%

profile of v1, /device:TPU:0, one launch (start us, length us, event | category | flops | bytes accessed | tf_op | source)
XLA Modules:
  0.0 145.0 jit_solution(16819453562813136352)
XLA Ops:
  6.5 0.0 copy-start
  6.5 0.0 all-gather.2.cloned.1.call-start
  6.5 0.7 all-gather.2.cloned.1.call-update
  7.3 1.6 %bitcast_dynamic-update-slice_fusion.7 = bf16[8,1,64,1024]{3,2,1,0:T(8,128)(2,1)} fusion(bf16[1,64,8192]{2,1,0:T(8,128)(2,1)} %param.9), kind=kLoop, calls=%fused_computation.16 | loop fusion | bytes 262144
  8.8 1.6 %bitcast_dynamic-update-slice_fusion.6 = bf16[8,1,64,1024]{3,2,1,0:T(8,128)(2,1)} fusion(bf16[8,1,64,1024]{3,2,1,0:T(8,128)(2,1)} %bitcast_dynamic-update-slice_fusion.7, bf16[1,64,8192]{2,1,0:T(8,128)(2,1)} %param.9), kind=kLoop, calls=%fused_computation.15 | loop fusion | bytes 262144
  10.4 1.6 %bitcast_dynamic-update-slice_fusion.5 = bf16[8,1,64,1024]{3,2,1,0:T(8,128)(2,1)} fusion(bf16[8,1,64,1024]{3,2,1,0:T(8,128)(2,1)} %bitcast_dynamic-update-slice_fusion.6, bf16[1,64,8192]{2,1,0:T(8,128)(2,1)} %param.9), kind=kLoop, calls=%fused_computation.14 | loop fusion | bytes 262144
  12.0 1.6 %bitcast_dynamic-update-slice_fusion.4 = bf16[8,1,64,1024]{3,2,1,0:T(8,128)(2,1)} fusion(bf16[8,1,64,1024]{3,2,1,0:T(8,128)(2,1)} %bitcast_dynamic-update-slice_fusion.5, bf16[1,64,8192]{2,1,0:T(8,128)(2,1)} %param.9), kind=kLoop, calls=%fused_computation.13 | loop fusion | bytes 262144
  13.5 1.6 %bitcast_dynamic-update-slice_fusion.3 = bf16[8,1,64,1024]{3,2,1,0:T(8,128)(2,1)} fusion(bf16[8,1,64,1024]{3,2,1,0:T(8,128)(2,1)} %bitcast_dynamic-update-slice_fusion.4, bf16[1,64,8192]{2,1,0:T(8,128)(2,1)} %param.9), kind=kLoop, calls=%fused_computation.12 | loop fusion | bytes 262144
  15.1 1.6 %bitcast_dynamic-update-slice_fusion.2 = bf16[8,1,64,1024]{3,2,1,0:T(8,128)(2,1)} fusion(bf16[8,1,64,1024]{3,2,1,0:T(8,128)(2,1)} %bitcast_dynamic-update-slice_fusion.3, bf16[1,64,8192]{2,1,0:T(8,128)(2,1)} %param.9), kind=kLoop, calls=%fused_computation.11 | loop fusion | bytes 262144
  16.7 1.6 %bitcast_dynamic-update-slice_fusion.1 = bf16[8,1,64,1024]{3,2,1,0:T(8,128)(2,1)} fusion(bf16[8,1,64,1024]{3,2,1,0:T(8,128)(2,1)} %bitcast_dynamic-update-slice_fusion.2, bf16[1,64,8192]{2,1,0:T(8,128)(2,1)} %param.9), kind=kLoop, calls=%fused_computation.10 | loop fusion | bytes 262144
  18.2 1.6 %bitcast_dynamic-update-slice_fusion = bf16[8,1,64,1024]{3,2,1,0:T(8,128)(2,1)} fusion(bf16[8,1,64,1024]{3,2,1,0:T(8,128)(2,1)} %bitcast_dynamic-update-slice_fusion.1, bf16[1,64,8192]{2,1,0:T(8,128)(2,1)} %param.9), kind=kLoop, calls=%fused_computation.9 | loop fusion | bytes 262144 | tf_op jit(solution)/shard_map/stack | solution.py:11
  19.8 5.2 %all-to-all-start = ((bf16[8,1,64,1024]{3,2,1,0:T(8,128)(2,1)}), bf16[8,1,64,1024]{3,2,1,0:T(8,128)(2,1)S(1)}, u32[]{:S(2)}, u32[]{:S(2)}) async-start(bf16[8,1,64,1024]{3,2,1,0:T(8,128)(2,1)} %bitcast_dynamic-update-slice_fusion), calls=%async_computation | async-start | bytes 2097152 | tf_op jit(solution)/shard_map/all_to_all | solution.py:12
  25.0 0.0 all-reduce.2.cloned.1.call-start
  25.1 0.9 select_reduce_fusion
  26.0 40.9 %all-gather.2.cloned.1.call-done = bf16[768,4096]{1,0:T(8,128)(2,1)} async-done(((bf16[768,512]{1,0:T(8,128)(2,1)}), bf16[768,4096]{1,0:T(8,128)(2,1)}) %all-gather.2.cloned.1.call-update) | async-done | bytes 6291472 | tf_op jit(solution)/shard_map/all_gather | solution.py:35
  66.9 0.0 copy-done
  66.9 5.4 %fusion.3 = bf16[6,64,128]{2,1,0:T(8,128)(2,1)} fusion(bf16[6,128,4096]{2,1,0:T(8,128)(2,1)} %bitcast.47, bf16[1,64,4096]{2,1,0:T(8,128)(2,1)S(1)} %copy-done, f32[6]{0:T(128)S(1)} %compare_convert_fusion), kind=kOutput, calls=%fused_computation.7 | convolution fusion | flops 402751488 | bytes 6914072 | tf_op jit(solution)/shard_map/btf,srf->bsrt/dot_general | solution.py:40
  72.3 0.0 all-reduce.2.cloned.1.call-update
  72.4 0.0 all-to-all-done
  72.4 0.6 gather_fusion
  73.0 51.6 %all-reduce.2.cloned.1.call-done = bf16[6,64,128]{2,1,0:T(8,128)(2,1)} async-done(((bf16[6,64,128]{2,1,0:T(8,128)(2,1)}), bf16[6,64,128]{2,1,0:T(8,128)(2,1)}) %all-reduce.2.cloned.1.call-update) | async-done | bytes 98320 | tf_op jit(solution)/shard_map/psum | solution.py:47
  124.6 1.5 %convolution_multiply_fusion = f32[6,128,1024]{2,1,0:T(8,128)S(1)} fusion(bf16[6,64,128]{2,1,0:T(8,128)(2,1)} %all-reduce.2.cloned.1.call-done, bf16[6,64,1024]{2,1,0:T(8,128)(2,1)S(1)} %gather_fusion), kind=kOutput, calls=%fused_computation.3 | convolution fusion | flops 101449728 | bytes 4030464 | tf_op jit(solution)/shard_map/brt,brc->btc/dot_general | solution.py:48
  126.1 12.1 %fusion = bf16[768,1024]{1,0:T(8,128)(2,1)} fusion(f32[6,128,1024]{2,1,0:T(8,128)S(1)} %convolution_multiply_fusion, bf16[768,4096]{1,0:T(8,128)(2,1)} %all-gather.2.cloned.1.call-done, bf16[4096,1024]{1,0:T(8,128)(2,1)} %param.7), kind=kOutput, calls=%fused_computation.2 | convolution fusion | flops 6444023808 | bytes 19398656 | tf_op jit(solution)/shard_map/dot_general | solution.py:36
  (3 shorter events, 0.0 us)
Async XLA Ops:
  6.5 60.4 %copy-start = (bf16[1,64,4096]{2,1,0:T(8,128)(2,1)S(1)}, bf16[1,64,4096]{2,1,0:T(8,128)(2,1)}, u32[]{:S(2)}) copy-start(bf16[1,64,4096]{2,1,0:T(8,128)(2,1)} %param.8) | copy-start | bytes 1572868
  6.5 60.4 %all-gather.2.cloned.1.call-start = ((), (), s32[]{:S(2)}) async-start(), calls=%async_computation.1 | async-start | bytes 7077888 | tf_op jit(solution)/shard_map/all_gather | solution.py:35
  19.8 52.6 %all-to-all-start = ((bf16[8,1,64,1024]{3,2,1,0:T(8,128)(2,1)}), bf16[8,1,64,1024]{3,2,1,0:T(8,128)(2,1)S(1)}, u32[]{:S(2)}, u32[]{:S(2)}) async-start(bf16[8,1,64,1024]{3,2,1,0:T(8,128)(2,1)} %bitcast_dynamic-update-slice_fusion), calls=%async_computation | async-start | bytes 2097152 | tf_op jit(solution)/shard_map/all_to_all | solution.py:12
  25.0 99.5 %all-reduce.2.cloned.1.call-start = ((), (), s32[]{:S(2)}) async-start(), calls=%async_computation.2 | async-start | bytes 196608 | tf_op jit(solution)/shard_map/psum | solution.py:47
Sparse Core Ops, SparseCore 0:
  9.2 57.6 all-gather.1
  72.5 52.0 all-reduce.1
